TPU v7x, 32 devices: a whole 2x2x4 slice. The times are simulated.
32 devices in a mesh: row: 8 (over y, x, core), col: 4 (over z).
Axes of the slice: x: 2, y: 2, z: 4, core: 2. Of those that a mesh axis runs over, the one named last changes fastest.
Arguments:
- hidden_in: bfloat16 [4096, 2048], P(('row', 'col')), may hold values from -6 to 6
- first_gain: float32 [2048], replicated, may hold values from 0.25 to 1.75
- query_weight: bfloat16 [2048, 4096], P(None, 'col'), may hold values from -0.125 to 0.125
- key_projection: bfloat16 [2048, 512], replicated, may hold values from -0.125 to 0.125
- value_projection: bfloat16 [2048, 512], replicated, may hold values from -0.125 to 0.125
- out_weight: bfloat16 [4096, 2048], P('col'), may hold values from -0.375 to 0.375
- query_gain: float32 [128], replicated, may hold values from 0.6 to 1.6, as said below
- key_gain: float32 [128], replicated, may hold values from 0.6 to 1.6, as said below
- second_gain: float32 [2048], replicated, may hold values from 0.25 to 1.75
- router_weight: bfloat16 [2048, 32], replicated, may hold values from -2 to 2
- gate_weight: bfloat16 [32, 2048, 768], P(('row', 'col')), may hold values from -0.125 to 0.125
- up_weight: bfloat16 [32, 2048, 768], P(('row', 'col')), may hold values from -0.125 to 0.125
- down_weight: bfloat16 [32, 768, 2048], P(('row', 'col')), may hold values from -0.21875 to 0.21875
- segments: int32 [8, 512], P('row'), may hold values from 0 to 2, never falling along the last dimension, each value on 1 to 480 neighbouring positions
- routes: int32 [4096, 8], P(('row', 'col')), may hold values from 0 to 31, all different within a row; in each aligned block of 128 rows (0 to 127, 128 to 255, ...) at most 36 rows name the same one
- cotangent: bfloat16 [4096, 2048], P(('row', 'col')), may hold values from -6 to 6
Outputs:
- block_out: bfloat16 [4096, 2048], P(('row', 'col'))
- input_grad: bfloat16 [4096, 2048], P(('row', 'col'))
- first_gain_grad: float32 [2048], replicated
- query_weight_grad: float32 [2048, 4096], P(None, 'col')
- key_weight_grad: float32 [2048, 512], replicated
- value_weight_grad: float32 [2048, 512], replicated
- out_weight_grad: float32 [4096, 2048], P('col')
- query_gain_grad: float32 [128], replicated
- key_gain_grad: float32 [128], replicated
- second_gain_grad: float32 [2048], replicated
- router_weight_grad: float32 [2048, 32], replicated
- gate_weight_grad: float32 [32, 2048, 768], P(('row', 'col'))
- up_weight_grad: float32 [32, 2048, 768], P(('row', 'col'))
- down_weight_grad: float32 [32, 768, 2048], P(('row', 'col'))
Inputs may be any that keep to these rules, and one draw needn't show every extreme that they name: In the rows of one device (128 tokens, aligned blocks) no expert is named by more than 36 routes, a bound that some block reaches; a token's 8 routes are different experts. `segments`: in each token group the ids start at 0 and never fall; every sequence has 1 to 480 tokens and one has exactly 480. `query_gain`: positive gains. `key_gain`: positive gains.
All inputs are finite; a program needn't handle non-finite values.
Results may differ from a plain program's by a relative error of at most 0.023.
Values may be sent and summed in bfloat16 or wider, within the bound.
A program may use at most 256 MiB of HBM per device.

v0:
```python
import jax
import jax.numpy as jnp
from jax import lax
from jax.sharding import PartitionSpec as P

QUERY_HEADS = 32
KEY_VALUE_HEADS = 4
HEAD_SIZE = 128
TOP = 8
EPSILON = 1e-06
THETA = 1000000.0
NEGATIVE = -1e30


def norm_rows(values, gain):
    return values * lax.rsqrt(jnp.mean(values * values, axis=-1, keepdims=True) + EPSILON) * gain


def positions(segment_row):
    index = jnp.arange(segment_row.shape[0], dtype=jnp.int32)
    begins = jnp.concatenate([jnp.ones((1,), dtype=jnp.bool_), segment_row[1:] != segment_row[:-1]])
    first = lax.cummax(jnp.where(begins, index, 0), axis=0)
    return index - first


def rope_tables(segment_row):
    half_width = HEAD_SIZE // 2
    freqs = THETA ** (-2.0 * jnp.arange(half_width, dtype=jnp.float32) / HEAD_SIZE)
    angles = positions(segment_row).astype(jnp.float32)[:, None] * freqs[None, :]
    return (jnp.cos(angles)[:, None, :], jnp.sin(angles)[:, None, :])


def head_prep(raw, gain, cosine, sine):
    normed_input = norm_rows(raw, gain)
    half_width = HEAD_SIZE // 2
    lower = normed_input[..., :half_width]
    upper = normed_input[..., half_width:]
    return jnp.concatenate([lower * cosine - upper * sine, upper * cosine + lower * sine], axis=-1)


def route_softmax(chosen):
    top_logit = jnp.max(chosen, axis=1, keepdims=True)
    raised = jnp.exp(chosen - top_logit)
    return raised / jnp.sum(raised, axis=1, keepdims=True)


def allowed_block(segment_row, row_begin, row_end):
    query_index = jnp.arange(row_begin, row_end, dtype=jnp.int32)
    key_index = jnp.arange(0, row_end, dtype=jnp.int32)
    causal = key_index[None, :] <= query_index[:, None]
    same_seq = segment_row[None, :row_end] == segment_row[row_begin:row_end, None]
    return causal & same_seq


def slot_numbers(flat_routes, expert_count):
    onehot = (flat_routes[:, None] == jnp.arange(expert_count, dtype=jnp.int32)[None, :]).astype(
        jnp.int32
    )
    earlier = jnp.cumsum(onehot, axis=0) - onehot
    return jnp.sum(earlier * onehot, axis=1)


def place_head(part_grad, full_shape, column_start):
    return lax.dynamic_update_slice_in_dim(
        jnp.zeros(full_shape, jnp.float32), part_grad, column_start, 1
    )


def trade(parcel):
    return lax.all_to_all(parcel, ("row", "col"), split_axis=0, concat_axis=0, tiled=True)


def shards(
    hidden_in,
    first_gain,
    query_weight,
    key_projection,
    value_projection,
    out_weight,
    query_gain,
    key_gain,
    second_gain,
    router_weight,
    gate_weight,
    up_weight,
    down_weight,
    segments,
    routes,
    cotangent,
):
    tok_rows = hidden_in.shape[0]
    model_width = hidden_in.shape[1]
    resid_in = hidden_in.astype(jnp.float32)
    normed_input, first_pull = jax.vjp(norm_rows, resid_in, first_gain)
    normed_low = normed_input.astype(jnp.bfloat16)
    gathered = lax.all_gather(normed_low, "col", axis=0, tiled=True)
    group_rows = gathered.shape[0]
    segment_row = segments[0]
    cosine, sine = rope_tables(segment_row)
    heads_here = query_weight.shape[1] // HEAD_SIZE
    group_heads = QUERY_HEADS // KEY_VALUE_HEADS
    kv_start = lax.axis_index("col") * heads_here // group_heads * HEAD_SIZE
    key_columns = lax.dynamic_slice_in_dim(key_projection, kv_start, HEAD_SIZE, 1)
    value_columns = lax.dynamic_slice_in_dim(value_projection, kv_start, HEAD_SIZE, 1)
    query_raw = jnp.dot(gathered, query_weight, preferred_element_type=jnp.float32).reshape(
        group_rows, heads_here, HEAD_SIZE
    )
    key_full = jnp.dot(gathered, key_columns, preferred_element_type=jnp.float32)
    value_full = jnp.dot(gathered, value_columns, preferred_element_type=jnp.float32)

    def prep_heads(raw, gain):
        return head_prep(raw, gain, cosine, sine)

    query_rotated, query_pull = jax.vjp(prep_heads, query_raw, query_gain)
    key_rotated, key_pull = jax.vjp(prep_heads, key_full[:, None, :], key_gain)
    query_low = query_rotated.astype(jnp.bfloat16)
    key_low = key_rotated[:, 0, :].astype(jnp.bfloat16)
    value_lowered = value_full.astype(jnp.bfloat16)
    block_rows = max(min(512, group_rows), group_rows // 8)
    score_scale = HEAD_SIZE ** (-0.5)
    pieces_out = []
    log_totals = []
    for row_begin in range(0, group_rows, block_rows):
        row_end = row_begin + block_rows
        scores = (
            jnp.einsum(
                "qhd,kd->hqk",
                query_low[row_begin:row_end],
                key_low[:row_end],
                preferred_element_type=jnp.float32,
            )
            * score_scale
        )
        scores = jnp.where(allowed_block(segment_row, row_begin, row_end)[None], scores, NEGATIVE)
        top_score = jnp.max(scores, axis=-1, keepdims=True)
        raised = jnp.exp(scores - top_score)
        row_total = jnp.sum(raised, axis=-1, keepdims=True)
        softmax_low = (raised / row_total).astype(jnp.bfloat16)
        pieces_out.append(
            jnp.einsum(
                "hqk,kd->qhd",
                softmax_low,
                value_lowered[:row_end],
                preferred_element_type=jnp.float32,
            )
        )
        log_totals.append(top_score + jnp.log(row_total))
    attention_output = (
        jnp.concatenate(pieces_out, axis=0)
        .reshape(group_rows, heads_here * HEAD_SIZE)
        .astype(jnp.bfloat16)
    )
    partial_branch = jnp.dot(attention_output, out_weight, preferred_element_type=jnp.float32)
    branch = lax.psum_scatter(
        partial_branch.astype(jnp.bfloat16), "col", scatter_dimension=0, tiled=True
    ).astype(jnp.float32)
    resid = resid_in + branch
    mixer_in, second_pull = jax.vjp(norm_rows, resid, second_gain)
    mixer_low = mixer_in.astype(jnp.bfloat16)
    logits = jnp.dot(mixer_low, router_weight, preferred_element_type=jnp.float32)
    expert_count = router_weight.shape[1]
    chosen = jnp.take_along_axis(logits, routes, axis=1)
    route_weights, route_pull = jax.vjp(route_softmax, chosen)
    capacity = max(2, tok_rows * TOP * 9 // (expert_count * 8))
    flat_routes = routes.reshape(-1)
    target = flat_routes * capacity + slot_numbers(flat_routes, expert_count)
    slot_rows = expert_count * capacity
    outgoing = (
        jnp.zeros((slot_rows, model_width), jnp.bfloat16)
        .at[target]
        .set(jnp.repeat(mixer_low, TOP, axis=0))
    )
    arrived = trade(outgoing.reshape(expert_count, capacity, model_width)).reshape(
        slot_rows, model_width
    )
    gate_value = jnp.dot(arrived, gate_weight[0], preferred_element_type=jnp.float32)
    up_value = jnp.dot(arrived, up_weight[0], preferred_element_type=jnp.float32)
    sigmoid_gate = jax.nn.sigmoid(gate_value)
    activated = (gate_value * sigmoid_gate * up_value).astype(jnp.bfloat16)
    expert_rows = jnp.dot(activated, down_weight[0], preferred_element_type=jnp.float32).astype(
        jnp.bfloat16
    )
    returned = trade(expert_rows.reshape(expert_count, capacity, model_width)).reshape(
        slot_rows, model_width
    )
    expert_out = returned[target].reshape(tok_rows, TOP, model_width)
    mixed = jnp.sum(route_weights[:, :, None] * expert_out, axis=1)
    block_out = (resid + mixed).astype(jnp.bfloat16)
    grad_out = cotangent.astype(jnp.float32)
    grad_expert_out = (
        (route_weights[:, :, None] * grad_out[:, None, :])
        .astype(jnp.bfloat16)
        .reshape(tok_rows * TOP, model_width)
    )
    grad_weights = jnp.sum(expert_out * grad_out[:, None, :], axis=-1)
    outgoing_grad = (
        jnp.zeros((slot_rows, model_width), jnp.bfloat16).at[target].set(grad_expert_out)
    )
    grad_arrived = trade(outgoing_grad.reshape(expert_count, capacity, model_width)).reshape(
        slot_rows, model_width
    )
    grad_act = jnp.einsum(
        "rd,fd->rf", grad_arrived, down_weight[0], preferred_element_type=jnp.float32
    )
    down_grad = jnp.einsum("rf,rd->fd", activated, grad_arrived, preferred_element_type=jnp.float32)
    grad_gate = (
        grad_act * up_value * sigmoid_gate * (1.0 + gate_value * (1.0 - sigmoid_gate))
    ).astype(jnp.bfloat16)
    grad_up = (grad_act * gate_value * sigmoid_gate).astype(jnp.bfloat16)
    gate_grad = jnp.einsum("rd,rf->df", arrived, grad_gate, preferred_element_type=jnp.float32)
    up_grad = jnp.einsum("rd,rf->df", arrived, grad_up, preferred_element_type=jnp.float32)
    grad_rows = jnp.einsum(
        "rf,df->rd", grad_gate, gate_weight[0], preferred_element_type=jnp.float32
    )
    grad_rows = (
        grad_rows
        + jnp.einsum("rf,df->rd", grad_up, up_weight[0], preferred_element_type=jnp.float32)
    ).astype(jnp.bfloat16)
    grad_back = trade(grad_rows.reshape(expert_count, capacity, model_width)).reshape(
        slot_rows, model_width
    )
    grad_mixer = jnp.sum(
        grad_back[target].reshape(tok_rows, TOP, model_width).astype(jnp.float32), axis=1
    )
    (grad_chosen,) = route_pull(grad_weights)
    picks = routes[:, :, None] == jnp.arange(expert_count, dtype=jnp.int32)[None, None, :]
    grad_logits = jnp.sum(jnp.where(picks, grad_chosen[:, :, None], 0.0), axis=1).astype(
        jnp.bfloat16
    )
    router_grad = jnp.einsum(
        "td,te->de", mixer_low, grad_logits, preferred_element_type=jnp.float32
    )
    grad_mixer = grad_mixer + jnp.einsum(
        "te,de->td", grad_logits, router_weight, preferred_element_type=jnp.float32
    )
    grad_second, second_gain_grad = second_pull(grad_mixer)
    grad_resid = grad_out + grad_second
    grad_branch = lax.all_gather(grad_resid.astype(jnp.bfloat16), "col", axis=0, tiled=True)
    out_grad = jnp.einsum(
        "gf,gd->fd", attention_output, grad_branch, preferred_element_type=jnp.float32
    )
    grad_attended = (
        jnp.einsum("gd,fd->gf", grad_branch, out_weight, preferred_element_type=jnp.float32)
        .astype(jnp.bfloat16)
        .reshape(group_rows, heads_here, HEAD_SIZE)
    )
    query_grads = []
    key_grad = jnp.zeros((group_rows, HEAD_SIZE), jnp.float32)
    value_grad = jnp.zeros((group_rows, HEAD_SIZE), jnp.float32)
    for block_index, row_begin in enumerate(range(0, group_rows, block_rows)):
        row_end = row_begin + block_rows
        scores = (
            jnp.einsum(
                "qhd,kd->hqk",
                query_low[row_begin:row_end],
                key_low[:row_end],
                preferred_element_type=jnp.float32,
            )
            * score_scale
        )
        scores = jnp.where(allowed_block(segment_row, row_begin, row_end)[None], scores, NEGATIVE)
        softmax_full = jnp.exp(scores - log_totals[block_index])
        softmax_low = softmax_full.astype(jnp.bfloat16)
        grad_soft = jnp.einsum(
            "qhd,kd->hqk",
            grad_attended[row_begin:row_end],
            value_lowered[:row_end],
            preferred_element_type=jnp.float32,
        )
        grad_scores = (
            softmax_full * (grad_soft - jnp.sum(softmax_full * grad_soft, axis=-1, keepdims=True))
        ).astype(jnp.bfloat16)
        query_grads.append(
            jnp.einsum(
                "hqk,kd->qhd", grad_scores, key_low[:row_end], preferred_element_type=jnp.float32
            )
            * score_scale
        )
        key_grad = key_grad.at[:row_end].add(
            jnp.einsum(
                "hqk,qhd->kd",
                grad_scores,
                query_low[row_begin:row_end],
                preferred_element_type=jnp.float32,
            )
            * score_scale
        )
        value_grad = value_grad.at[:row_end].add(
            jnp.einsum(
                "hqk,qhd->kd",
                softmax_low,
                grad_attended[row_begin:row_end],
                preferred_element_type=jnp.float32,
            )
        )
    grad_query_raw, query_gain_grad = query_pull(jnp.concatenate(query_grads, axis=0))
    grad_key_raw, key_gain_grad = key_pull(key_grad[:, None, :])
    query_grad_low = grad_query_raw.reshape(group_rows, heads_here * HEAD_SIZE).astype(jnp.bfloat16)
    key_grad_low = grad_key_raw[:, 0, :].astype(jnp.bfloat16)
    value_grad_low = value_grad.astype(jnp.bfloat16)
    grad_normed_part = jnp.einsum(
        "gf,df->gd", query_grad_low, query_weight, preferred_element_type=jnp.float32
    )
    grad_normed_part = grad_normed_part + jnp.einsum(
        "gf,df->gd", key_grad_low, key_columns, preferred_element_type=jnp.float32
    )
    grad_normed_part = grad_normed_part + jnp.einsum(
        "gf,df->gd", value_grad_low, value_columns, preferred_element_type=jnp.float32
    )
    grad_normed = lax.psum_scatter(
        grad_normed_part.astype(jnp.bfloat16), "col", scatter_dimension=0, tiled=True
    ).astype(jnp.float32)
    grad_first, first_gain_grad = first_pull(grad_normed)
    input_grad = (grad_resid + grad_first).astype(jnp.bfloat16)
    query_grad = jnp.einsum(
        "gd,gf->df", gathered, query_grad_low, preferred_element_type=jnp.float32
    )
    key_head_grad = jnp.einsum(
        "gd,gf->df", gathered, key_grad_low, preferred_element_type=jnp.float32
    )
    value_head_grad = jnp.einsum(
        "gd,gf->df", gathered, value_grad_low, preferred_element_type=jnp.float32
    )
    key_weight_part = place_head(key_head_grad, key_projection.shape, kv_start)
    value_weight_part = place_head(value_head_grad, value_projection.shape, kv_start)
    query_grad, out_grad = (
        lax.psum(query_grad.astype(jnp.bfloat16), "row").astype(jnp.float32),
        lax.psum(out_grad.astype(jnp.bfloat16), "row").astype(jnp.float32),
    )
    (
        router_grad,
        key_weight_part,
        value_weight_part,
        first_gain_grad,
        second_gain_grad,
        query_gain_grad,
        key_gain_grad,
    ) = lax.psum(
        (
            router_grad,
            key_weight_part,
            value_weight_part,
            first_gain_grad,
            second_gain_grad,
            query_gain_grad,
            key_gain_grad,
        ),
        ("row", "col"),
    )
    return (
        block_out,
        input_grad,
        first_gain_grad,
        query_grad,
        key_weight_part,
        value_weight_part,
        out_grad,
        query_gain_grad,
        key_gain_grad,
        second_gain_grad,
        router_grad,
        gate_grad[None],
        up_grad[None],
        down_grad[None],
    )


def solution(mesh):
    placed = (
        P(("row", "col"), None),
        P(),
        P(None, "col"),
        P(),
        P(),
        P("col", None),
        P(),
        P(),
        P(),
        P(),
        P(("row", "col"), None, None),
        P(("row", "col"), None, None),
        P(("row", "col"), None, None),
        P("row", None),
        P(("row", "col"), None),
        P(("row", "col"), None),
    )
    return jax.shard_map(
        shards,
        mesh=mesh,
        in_specs=placed,
        out_specs=(
            P(("row", "col"), None),
            P(("row", "col"), None),
            P(),
            P(None, "col"),
            P(),
            P(),
            P("col", None),
            P(),
            P(),
            P(),
            P(),
            P(("row", "col"), None, None),
            P(("row", "col"), None, None),
            P(("row", "col"), None, None),
        ),
        check_vma=False,
    )
```

profile of v0, /device:TPU:0, one launch (start us, length us, event | category | flops | bytes accessed | tf_op | source)
XLA Modules:
  0.0 1155.9 jit_solution(15615479029955595789)
XLA Ops:
  16.9 43.5 %all-gather.3.cloned.1.call-done = bf16[512,2048]{1,0:T(8,128)(2,1)} async-done(((bf16[128,2048]{1,0:T(8,128)(2,1)}), bf16[512,2048]{1,0:T(8,128)(2,1)}) %all-gather.3.cloned.1.call-update) | async-done | bytes 2097168 | tf_op jit(solution)/shard_map/all_gather | solution.py:96
  90.3 9.0 reduce-window.19
  99.8 32.6 %reduce-scatter.3.cloned.1.call-done = bf16[128,2048]{1,0:T(8,128)(2,1)} async-done(((bf16[512,2048]{1,0:T(8,128)(2,1)}), bf16[128,2048]{1,0:T(8,128)(2,1)}) %reduce-scatter.3.cloned.1.call-update) | async-done | bytes 524304 | tf_op jit(solution)/shard_map/reduce_scatter | solution.py:154
  136.1 10.2 scatter_custom_fusion
  168.6 10.2 scatter_custom_fusion.1
  186.0 85.9 %all-to-all-done = bf16[32,36,2048]{2,1,0:T(8,128)(2,1)} async-done(((bf16[32,36,2048]{2,1,0:T(8,128)(2,1)}), bf16[32,36,2048]{2,1,0:T(8,128)(2,1)}, u32[]{:S(2)}, u32[]{:S(2)}) %all-to-all-start) | async-done | bytes 4718624 | tf_op jit(solution)/shard_map/all_to_all | solution.py:70
  278.4 7.2 reshape.558
  285.6 9.1 fusion.26
  300.4 92.4 %all-to-all-done.2 = bf16[32,36,2048]{2,1,0:T(8,128)(2,1)} async-done(((bf16[32,36,2048]{2,1,0:T(8,128)(2,1)}), bf16[32,36,2048]{2,1,0:T(8,128)(2,1)}, u32[]{:S(2)}, u32[]{:S(2)}) %all-to-all-start.2) | async-done | bytes 4718624 | tf_op jit(solution)/shard_map/all_to_all | solution.py:70
  392.8 7.2 reshape.562
  400.1 9.6 multiply_convert_fusion
  447.2 100.3 %all-to-all-done.3 = bf16[32,36,2048]{2,1,0:T(8,128)(2,1)} async-done(((bf16[32,36,2048]{2,1,0:T(8,128)(2,1)}), bf16[32,36,2048]{2,1,0:T(8,128)(2,1)}, u32[]{:S(2)}, u32[]{:S(2)}) %all-to-all-start.3) | async-done | bytes 4718624 | tf_op jit(solution)/shard_map/all_to_all | solution.py:70
  553.9 7.2 reshape.564
  561.2 11.8 %gather_fusion.1 = bf16[1024,2048]{1,0:T(8,128)(2,1)} fusion(bf16[1152,2048]{1,0:T(8,128)(2,1)} %reshape.564, s32[1024]{0:T(1024)S(1)} %broadcast_clamp_fusion), kind=kCustom, calls=%fused_computation.1 | custom fusion | bytes 8392704 | tf_op jit(solution)/shard_map/gather | solution.py:223
  578.9 89.3 %all-to-all-done.1 = bf16[32,36,2048]{2,1,0:T(8,128)(2,1)} async-done(((bf16[32,36,2048]{2,1,0:T(8,128)(2,1)}), bf16[32,36,2048]{2,1,0:T(8,128)(2,1)}, u32[]{:S(2)}, u32[]{:S(2)}) %all-to-all-start.1) | async-done | bytes 4718624 | tf_op jit(solution)/shard_map/all_to_all | solution.py:70
  675.5 11.8 %gather_fusion = bf16[1024,2048]{1,0:T(8,128)(2,1)} fusion(bf16[1152,2048]{1,0:T(8,128)(2,1)} %reshape.560, s32[1024]{0:T(1024)S(1)} %broadcast_clamp_fusion), kind=kCustom, calls=%fused_computation | custom fusion | bytes 8392704 | tf_op jit(solution)/shard_map/gather | solution.py:186
  697.5 47.2 %all-gather.5.cloned.1.call-done = bf16[512,2048]{1,0:T(8,128)(2,1)} async-done(((bf16[128,2048]{1,0:T(8,128)(2,1)}), bf16[512,2048]{1,0:T(8,128)(2,1)}) %all-gather.5.cloned.1.call-update) | async-done | bytes 2097168 | tf_op jit(solution)/shard_map/all_gather | solution.py:238
  811.5 8.7 convolution_bitcast_fusion.2
  820.2 8.6 convolution_bitcast_fusion.1
  828.9 8.5 convolution_bitcast_fusion
  837.4 67.9 %all-reduce.12.cloned.1.call-done = (bf16[2048,1024]{1,0:T(8,128)(2,1)}, bf16[1024,2048]{1,0:T(8,128)(2,1)}) async-done(((bf16[2048,1024]{1,0:T(8,128)(2,1)}, bf16[1024,2048]{1,0:T(8,128)(2,1)}), (bf16[2048,1024]{1,0:T(8,128)(2,1)}, bf16[1024,2048]{1,0:T(8,128)(2,1)})) %all-reduce.12.cloned.1.call-update) | async-done | bytes 8388624 | tf_op jit(solution)/shard_map/psum | solution.py:327
  916.6 34.6 %reduce-scatter.5.cloned.1.call-done = bf16[128,2048]{1,0:T(8,128)(2,1)} async-done(((bf16[512,2048]{1,0:T(8,128)(2,1)}), bf16[128,2048]{1,0:T(8,128)(2,1)}) %reduce-scatter.5.cloned.1.call-update) | async-done | bytes 524304 | tf_op jit(solution)/shard_map/reduce_scatter | solution.py:310
  952.8 41.5 %all-reduce.4 = (f32[2048]{0:T(1024)}, f32[128]{0:T(128)}, f32[128]{0:T(128)}, f32[2048]{0:T(1024)}) all-reduce(f32[2048]{0:T(1024)S(1)} %get-tuple-element.60, f32[128]{0:T(128)S(1)} %copy-done.72, f32[128]{0:T(128)S(1)} %copy-done.71, f32[2048]{0:T(1024)S(1)} %copy-done.55), channel_id=1, replica_groups=mesh['row'=8,'col'=4] {'row','col'}, use_global_device_ids=true, to_apply=%region_30.31 | all-reduce | flops 4352 | bytes 34816 | tf_op jit(solution)/shard_map/psum | solution.py:338
  997.6 143.4 %all-reduce.10.cloned.1.call-done = (f32[2048,512]{1,0:T(8,128)}, f32[2048,512]{1,0:T(8,128)}, f32[2048,32]{0,1:T(8,128)}) async-done(((f32[2048,512]{1,0:T(8,128)}, f32[2048,512]{1,0:T(8,128)}, f32[2048,32]{0,1:T(8,128)}), (f32[2048,512]{1,0:T(8,128)}, f32[2048,512]{1,0:T(8,128)}, f32[2048,32]{0,1:T(8,128)})) %all-reduce.10.cloned.1.call-update) | async-done | bytes 8650768 | tf_op jit(solution)/shard_map/psum | solution.py:338
  (310 shorter events, 242.1 us)
Async XLA Ops:
  7.2 392.9 %copy-start = (bf16[1,768,2048]{2,1,0:T(8,128)(2,1)S(1)}, bf16[1,768,2048]{2,1,0:T(8,128)(2,1)}, u32[]{:S(2)}) copy-start(bf16[1,768,2048]{2,1,0:T(8,128)(2,1)} %param.36) | copy-start | bytes 9437188
  7.2 53.2 %all-gather.3.cloned.1.call-start = ((), (), s32[]{:S(2)}) async-start(), calls=%async_computation.6 | async-start | bytes 2621440 | tf_op jit(solution)/shard_map/all_gather | solution.py:96
  11.8 120.6 %reduce-scatter.3.cloned.1.call-start = ((), (), s32[]{:S(2)}) async-start(), calls=%async_computation.7 | async-start | bytes 2621440 | tf_op jit(solution)/shard_map/reduce_scatter | solution.py:154
  13.3 59.3 %copy-start.62 = (f32[64]{0:T(128)}, f32[64]{0:T(128)S(1)}, u32[]{:S(2)}) copy-start(f32[64]{0:T(128)S(1)} %multiply_power_fusion) | copy-start | bytes 772
  13.5 59.1 %copy-start.50 = (f32[512]{0:T(512)}, f32[512]{0:T(512)S(1)}, u32[]{:S(2)}) copy-start(f32[512]{0:T(512)S(1)} %fusion.94) | copy-start | bytes 6148
  16.9 57.8 %copy-start.25 = (f32[512,64]{1,0:T(8,128)}, f32[512,64]{1,0:T(8,128)S(1)}, u32[]{:S(2)}) copy-start(f32[512,64]{1,0:T(8,128)S(1)} %get-tuple-element.91) | copy-start | bytes 393220
  133.9 562.0 %copy-start.58 = (f32[128]{0:T(128)}, f32[128]{0:T(128)S(1)}, u32[]{:S(2)}) copy-start(f32[128]{0:T(128)S(1)} %fusion.101) | copy-start | bytes 1540
  153.5 118.3 %all-to-all-start = ((bf16[32,36,2048]{2,1,0:T(8,128)(2,1)}), bf16[32,36,2048]{2,1,0:T(8,128)(2,1)}, u32[]{:S(2)}, u32[]{:S(2)}) async-start(bf16[32,36,2048]{2,1,0:T(8,128)(2,1)} %reshape.557), calls=%async_computation.1 | async-start | bytes 10485760 | tf_op jit(solution)/shard_map/all_to_all | solution.py:70
  271.9 120.9 %all-to-all-start.2 = ((bf16[32,36,2048]{2,1,0:T(8,128)(2,1)}), bf16[32,36,2048]{2,1,0:T(8,128)(2,1)}, u32[]{:S(2)}, u32[]{:S(2)}) async-start(bf16[32,36,2048]{2,1,0:T(8,128)(2,1)} %reshape.561), calls=%async_computation.3 | async-start | bytes 10485760 | tf_op jit(solution)/shard_map/all_to_all | solution.py:70
  426.7 120.8 %all-to-all-start.3 = ((bf16[32,36,2048]{2,1,0:T(8,128)(2,1)}), bf16[32,36,2048]{2,1,0:T(8,128)(2,1)}, u32[]{:S(2)}, u32[]{:S(2)}) async-start(bf16[32,36,2048]{2,1,0:T(8,128)(2,1)} %reshape.563), calls=%async_computation.4 | async-start | bytes 10485760 | tf_op jit(solution)/shard_map/all_to_all | solution.py:70
  547.5 120.8 %all-to-all-start.1 = ((bf16[32,36,2048]{2,1,0:T(8,128)(2,1)}), bf16[32,36,2048]{2,1,0:T(8,128)(2,1)}, u32[]{:S(2)}, u32[]{:S(2)}) async-start(bf16[32,36,2048]{2,1,0:T(8,128)(2,1)} %reshape.559), calls=%async_computation.2 | async-start | bytes 10485760 | tf_op jit(solution)/shard_map/all_to_all | solution.py:70
  553.9 190.8 %all-gather.5.cloned.1.call-start = ((), (), s32[]{:S(2)}) async-start(), calls=%async_computation.8 | async-start | bytes 2621440 | tf_op jit(solution)/shard_map/all_gather | solution.py:238
  693.5 56.5 %copy-start.48 = (bf16[128,32]{0,1:T(8,128)(2,1)}, bf16[128,32]{0,1:T(8,128)(2,1)S(1)}, u32[]{:S(2)}) copy-start(bf16[128,32]{0,1:T(8,128)(2,1)S(1)} %select_reduce_fusion) | copy-start | bytes 24580
  695.9 54.1 %copy-start.11 = (f32[128,2048]{1,0:T(8,128)}, f32[128,2048]{1,0:T(8,128)S(1)}, u32[]{:S(2)}) copy-start(f32[128,2048]{1,0:T(8,128)S(1)} %get-tuple-element.97) | copy-start | bytes 3145732
  695.9 54.1 %copy-start.69 = (f32[128]{0:T(128)}, f32[128]{0:T(128)S(1)}, u32[]{:S(2)}) copy-start(f32[128]{0:T(128)S(1)} %multiply_multiply_fusion.3) | copy-start | bytes 1540
  697.2 208.0 %all-reduce.12.cloned.1.call-start = ((), (), s32[]{:S(2)}) async-start(), calls=%async_computation.11 | async-start | bytes 16777216 | tf_op jit(solution)/shard_map/psum | solution.py:327
  780.1 171.0 %reduce-scatter.5.cloned.1.call-start = ((), (), s32[]{:S(2)}) async-start(), calls=%async_computation.9 | async-start | bytes 2621440 | tf_op jit(solution)/shard_map/reduce_scatter | solution.py:310
  799.1 341.8 %all-reduce.10.cloned.1.call-start = ((), (), s32[]{:S(2)}) async-start(), calls=%async_computation.10 | async-start | bytes 17301504 | tf_op jit(solution)/shard_map/psum | solution.py:338
  912.1 82.3 %copy-start.74 = (f32[128]{0:T(128)S(1)}, f32[128]{0:T(128)}, u32[]{:S(2)}) copy-start(f32[128]{0:T(128)} %copy-done.73) | copy-start | bytes 1540
  912.1 82.3 %copy-start.12 = (f32[128,2048]{1,0:T(8,128)S(1)}, f32[128,2048]{1,0:T(8,128)}, u32[]{:S(2)}) copy-start(f32[128,2048]{1,0:T(8,128)} %copy-done.11) | copy-start | bytes 3145732
  912.1 82.3 %copy-start.17 = (bf16[128,2048]{1,0:T(8,128)(2,1)S(1)}, bf16[128,2048]{1,0:T(8,128)(2,1)}, u32[]{:S(2)}) copy-start(bf16[128,2048]{1,0:T(8,128)(2,1)} %param.39) | copy-start | bytes 1572868
  912.1 82.3 %copy-start.45 = (f32[2048]{0:T(1024)S(1)}, f32[2048]{0:T(1024)}, u32[]{:S(2)}) copy-start(f32[2048]{0:T(1024)} %param.32) | copy-start | bytes 24580
  912.1 82.3 %copy-start.59 = (f32[128]{0:T(128)S(1)}, f32[128]{0:T(128)}, u32[]{:S(2)}) copy-start(f32[128]{0:T(128)} %copy-done.58) | copy-start | bytes 1540
  912.1 82.3 %copy-start.70 = (f32[128]{0:T(128)S(1)}, f32[128]{0:T(128)}, u32[]{:S(2)}) copy-start(f32[128]{0:T(128)} %copy-done.69) | copy-start | bytes 1540
  (74 other events, 597.4 us)
Sparse Core Ops, SparseCore 0:
  11.9 48.3 all-gather.2
  89.9 42.5 reduce-scatter.2
  697.3 47.2 all-gather.4
  780.2 125.0 all-reduce.11
  907.4 43.7 reduce-scatter.4
  958.4 182.5 all-reduce.9
where the time goes:
time: 1160 us
  waiting for transfers between devices  737 us (64%)
  matrix products  134 us (12%)
  local copies, waits for them, and re-layouts  125 us (11%)
  other arithmetic  77.6 us (7%)
  blocking collectives  41.5 us (4%)
  starting transfers between devices  24.1 us (2%)
  between operations  15.9 us (1%)
    all_to_all x4, waiting for transfers between devices, trade(): lax.all_to_all(parcel, ('row', 'col'), split_axis=0, concat_axis=0, tiled...  368 us
    psum x1, waiting for transfers between devices, shards(): lax.psum((router_grad, key_weight_part, value_weight_part, first_gain_gra...  143 us
    psum x1, waiting for transfers between devices, shards(): lax.psum(query_grad.astype(jnp.bfloat16), 'row').astype(jnp.float32)  67.9 us
    all_gather x1, waiting for transfers between devices, shards(): lax.all_gather(grad_resid.astype(jnp.bfloat16), 'col', axis=0, tiled=True)  47.2 us
    all_gather x1, waiting for transfers between devices, shards(): gathered = lax.all_gather(normed_low, 'col', axis=0, tiled=True)  43.5 us
    psum x1, blocking collectives, shards(): lax.psum((router_grad, key_weight_part, value_weight_part, first_gain_gra...  41.5 us
    reduce_scatter x1, waiting for transfers between devices, shards(): lax.psum_scatter(grad_normed_part.astype(jnp.bfloat16), 'col', scatter_di...  34.6 us
    reduce_scatter x1, waiting for transfers between devices, shards(): lax.psum_scatter(partial_branch.astype(jnp.bfloat16), 'col', scatter_dime...  32.6 us
  transfers between devices with their start and end apart: 10, of which 10 were waited for; matrix products, arithmetic and copies ran while one was open for 15% of the time, Pallas kernels for 0%

commit v1 on v0

--- a/solution.py
+++ b/solution.py
@@ -10,6 +10,12 @@
 EPSILON = 1e-06
 THETA = 1000000.0
 NEGATIVE = -1e30
+
+
+def gather_and_add(x, axis):
+    parts = lax.all_gather(x, axis, axis=0, tiled=False)
+    total = parts.sum(axis=0)
+    return total
 
 
 def norm_rows(values, gain):
@@ -324,7 +330,7 @@
     key_weight_part = place_head(key_head_grad, key_projection.shape, kv_start)
     value_weight_part = place_head(value_head_grad, value_projection.shape, kv_start)
     query_grad, out_grad = (
-        lax.psum(query_grad.astype(jnp.bfloat16), "row").astype(jnp.float32),
+        gather_and_add(query_grad.astype(jnp.bfloat16), "row").astype(jnp.float32),
         lax.psum(out_grad.astype(jnp.bfloat16), "row").astype(jnp.float32),
     )
     (

time: 1160 us -> 1280 us (1.10)
  waiting for transfers between devices: 737 us -> 838 us
  other arithmetic: 77.6 us -> 95.1 us
    all_gather x0 -> x1, waiting for transfers between devices: none -> 117 us  [gather_and_add(): parts = lax.all_gather(x, axis, axis=0, tiled=False)]
    psum x1, waiting for transfers between devices: 67.9 us -> 21.7 us  [shards(): lax.psum(out_grad.astype(jnp.bfloat16), 'row').astype(jnp.float32)]
    psum x1, waiting for transfers between devices: 143 us -> 169 us  [shards(): lax.psum((router_grad, key_weight_part, value_weight_part, first_gain_gra...]
    reduce_sum x0 -> x1, other arithmetic: none -> 14.5 us  [gather_and_add(): total = parts.sum(axis=0)]
  transfers between devices with their start and end apart: 10 -> 11, of which waited for: 10 -> 11; matrix products, arithmetic and copies ran while one was open for 15% -> 15% of each run, Pallas kernels for 0% -> 0%
where the time goes in v1:
time: 1280 us; the launch traced here: 1270 us
  waiting for transfers between devices  838 us (65%)
  matrix products  134 us (10%)
  local copies, waits for them, and re-layouts  126 us (10%)
  other arithmetic  95.1 us (7%)
  blocking collectives  40.9 us (3%)
  starting transfers between devices  24.1 us (2%)
  between operations  15.9 us (1%)
    all_to_all x4, waiting for transfers between devices, trade(): lax.all_to_all(parcel, ('row', 'col'), split_axis=0, concat_axis=0, tiled...  368 us
    psum x1, waiting for transfers between devices, shards(): lax.psum((router_grad, key_weight_part, value_weight_part, first_gain_gra...  169 us
    all_gather x1, waiting for transfers between devices, gather_and_add(): parts = lax.all_gather(x, axis, axis=0, tiled=False)  117 us
    all_gather x1, waiting for transfers between devices, shards(): lax.all_gather(grad_resid.astype(jnp.bfloat16), 'col', axis=0, tiled=True)  47.2 us
    all_gather x1, waiting for transfers between devices, shards(): gathered = lax.all_gather(normed_low, 'col', axis=0, tiled=True)  43.5 us
    psum x1, blocking collectives, shards(): lax.psum((router_grad, key_weight_part, value_weight_part, first_gain_gra...  40.9 us
    reduce_scatter x1, waiting for transfers between devices, shards(): lax.psum_scatter(grad_normed_part.astype(jnp.bfloat16), 'col', scatter_di...  39.2 us
    reduce_scatter x1, waiting for transfers between devices, shards(): lax.psum_scatter(partial_branch.astype(jnp.bfloat16), 'col', scatter_dime...  32.6 us
  transfers between devices with their start and end apart: 11, of which 11 were waited for; matrix products, arithmetic and copies ran while one was open for 15% of the time, Pallas kernels for 0%

profile of v1, /device:TPU:0, one launch (start us, length us, event | category | flops | bytes accessed | tf_op | source)
XLA Modules:
  0.0 1273.6 jit_solution(1445782385569337055)
XLA Ops:
  16.8 43.5 %all-gather.5.cloned.1.call-done = bf16[512,2048]{1,0:T(8,128)(2,1)} async-done(((bf16[128,2048]{1,0:T(8,128)(2,1)}), bf16[512,2048]{1,0:T(8,128)(2,1)}) %all-gather.5.cloned.1.call-update) | async-done | bytes 2097168 | tf_op jit(solution)/shard_map/all_gather | solution.py:102
  90.2 9.0 reduce-window.19
  99.7 32.6 %reduce-scatter.3.cloned.1.call-done = bf16[128,2048]{1,0:T(8,128)(2,1)} async-done(((bf16[512,2048]{1,0:T(8,128)(2,1)}), bf16[128,2048]{1,0:T(8,128)(2,1)}) %reduce-scatter.3.cloned.1.call-update) | async-done | bytes 524304 | tf_op jit(solution)/shard_map/reduce_scatter | solution.py:160
  136.1 10.2 scatter_custom_fusion
  168.5 10.2 scatter_custom_fusion.1
  185.8 85.9 %all-to-all-done = bf16[32,36,2048]{2,1,0:T(8,128)(2,1)} async-done(((bf16[32,36,2048]{2,1,0:T(8,128)(2,1)}), bf16[32,36,2048]{2,1,0:T(8,128)(2,1)}, u32[]{:S(2)}, u32[]{:S(2)}) %all-to-all-start) | async-done | bytes 4718624 | tf_op jit(solution)/shard_map/all_to_all | solution.py:76
  285.5 9.1 fusion.26
  300.3 92.4 %all-to-all-done.2 = bf16[32,36,2048]{2,1,0:T(8,128)(2,1)} async-done(((bf16[32,36,2048]{2,1,0:T(8,128)(2,1)}), bf16[32,36,2048]{2,1,0:T(8,128)(2,1)}, u32[]{:S(2)}, u32[]{:S(2)}) %all-to-all-start.2) | async-done | bytes 4718624 | tf_op jit(solution)/shard_map/all_to_all | solution.py:76
  392.7 7.2 reshape.562
  399.9 9.6 multiply_convert_fusion
  447.0 100.3 %all-to-all-done.3 = bf16[32,36,2048]{2,1,0:T(8,128)(2,1)} async-done(((bf16[32,36,2048]{2,1,0:T(8,128)(2,1)}), bf16[32,36,2048]{2,1,0:T(8,128)(2,1)}, u32[]{:S(2)}, u32[]{:S(2)}) %all-to-all-start.3) | async-done | bytes 4718624 | tf_op jit(solution)/shard_map/all_to_all | solution.py:76
  561.0 11.8 gather_fusion.1
  578.8 89.3 %all-to-all-done.1 = bf16[32,36,2048]{2,1,0:T(8,128)(2,1)} async-done(((bf16[32,36,2048]{2,1,0:T(8,128)(2,1)}), bf16[32,36,2048]{2,1,0:T(8,128)(2,1)}, u32[]{:S(2)}, u32[]{:S(2)}) %all-to-all-start.1) | async-done | bytes 4718624 | tf_op jit(solution)/shard_map/all_to_all | solution.py:76
  675.3 11.8 gather_fusion
  697.3 47.2 %all-gather.7.cloned.1.call-done = bf16[512,2048]{1,0:T(8,128)(2,1)} async-done(((bf16[128,2048]{1,0:T(8,128)(2,1)}), bf16[512,2048]{1,0:T(8,128)(2,1)}) %all-gather.7.cloned.1.call-update) | async-done | bytes 2097168 | tf_op jit(solution)/shard_map/all_gather | solution.py:244
  812.7 8.5 convolution_bitcast_fusion.2
  821.2 8.5 convolution_bitcast_fusion.1
  829.8 8.5 convolution_bitcast_fusion
  838.4 21.7 %all-reduce.9.cloned.1.call-done = bf16[1024,2048]{1,0:T(8,128)(2,1)} async-done(((bf16[1024,2048]{1,0:T(8,128)(2,1)}), bf16[1024,2048]{1,0:T(8,128)(2,1)}) %all-reduce.9.cloned.1.call-update) | async-done | bytes 4194320 | tf_op jit(solution)/shard_map/psum | solution.py:334
  866.8 39.2 %reduce-scatter.5.cloned.1.call-done = bf16[128,2048]{1,0:T(8,128)(2,1)} async-done(((bf16[512,2048]{1,0:T(8,128)(2,1)}), bf16[128,2048]{1,0:T(8,128)(2,1)}) %reduce-scatter.5.cloned.1.call-update) | async-done | bytes 524304 | tf_op jit(solution)/shard_map/reduce_scatter | solution.py:316
  907.6 40.9 %all-reduce.4 = (f32[2048]{0:T(1024)}, f32[128]{0:T(128)}, f32[128]{0:T(128)}, f32[2048]{0:T(1024)}) all-reduce(f32[2048]{0:T(1024)S(1)} %get-tuple-element.60, f32[128]{0:T(128)S(1)} %copy-done.71, f32[128]{0:T(128)S(1)} %copy-done.70, f32[2048]{0:T(1024)S(1)} %copy-done.54), channel_id=1, replica_groups=mesh['row'=8,'col'=4] {'row','col'}, use_global_device_ids=true, to_apply=%region_30.31 | all-reduce | flops 4352 | bytes 34816 | tf_op jit(solution)/shard_map/psum | solution.py:344
  951.8 117.2 %all-gather.9.cloned.1.call-done = bf16[16384,1024]{1,0:T(8,128)(2,1)} async-done(((bf16[2048,1024]{1,0:T(8,128)(2,1)}), bf16[16384,1024]{1,0:T(8,128)(2,1)}) %all-gather.9.cloned.1.call-update) | async-done | bytes 33554448 | tf_op jit(solution)/shard_map/all_gather | solution.py:16
  1068.9 14.5 %reduce_sum.282 = bf16[2048,1024]{1,0:T(8,128)(2,1)} reduce(bf16[8,2048,1024]{2,1,0:T(8,128)(2,1)} %bitcast.203, bf16[]{:T(256)} %constant.168.clone.1), dimensions={0}, to_apply=%region_31.32 | reduce | flops 14680064 | bytes 37748736 | tf_op jit(solution)/shard_map/reduce_sum | solution.py:17
  1090.1 168.5 %all-reduce.11.cloned.1.call-done = (f32[2048,512]{1,0:T(8,128)}, f32[2048,512]{1,0:T(8,128)}, f32[2048,32]{0,1:T(8,128)}) async-done(((f32[2048,512]{1,0:T(8,128)}, f32[2048,512]{1,0:T(8,128)}, f32[2048,32]{0,1:T(8,128)}), (f32[2048,512]{1,0:T(8,128)}, f32[2048,512]{1,0:T(8,128)}, f32[2048,32]{0,1:T(8,128)})) %all-reduce.11.cloned.1.call-update) | async-done | bytes 8650768 | tf_op jit(solution)/shard_map/psum | solution.py:344
  (312 shorter events, 259.8 us)
Async XLA Ops:
  7.2 392.7 %copy-start = (bf16[1,768,2048]{2,1,0:T(8,128)(2,1)S(1)}, bf16[1,768,2048]{2,1,0:T(8,128)(2,1)}, u32[]{:S(2)}) copy-start(bf16[1,768,2048]{2,1,0:T(8,128)(2,1)} %param.36) | copy-start | bytes 9437188
  7.2 53.1 %all-gather.5.cloned.1.call-start = ((), (), s32[]{:S(2)}) async-start(), calls=%async_computation.6 | async-start | bytes 2621440 | tf_op jit(solution)/shard_map/all_gather | solution.py:102
  11.8 120.6 %reduce-scatter.3.cloned.1.call-start = ((), (), s32[]{:S(2)}) async-start(), calls=%async_computation.7 | async-start | bytes 2621440 | tf_op jit(solution)/shard_map/reduce_scatter | solution.py:160
  133.8 561.9 %copy-start.57 = (f32[128]{0:T(128)}, f32[128]{0:T(128)S(1)}, u32[]{:S(2)}) copy-start(f32[128]{0:T(128)S(1)} %fusion.101) | copy-start | bytes 1540
  153.5 118.3 %all-to-all-start = ((bf16[32,36,2048]{2,1,0:T(8,128)(2,1)}), bf16[32,36,2048]{2,1,0:T(8,128)(2,1)}, u32[]{:S(2)}, u32[]{:S(2)}) async-start(bf16[32,36,2048]{2,1,0:T(8,128)(2,1)} %reshape.557), calls=%async_computation.1 | async-start | bytes 10485760 | tf_op jit(solution)/shard_map/all_to_all | solution.py:76
  271.8 120.9 %all-to-all-start.2 = ((bf16[32,36,2048]{2,1,0:T(8,128)(2,1)}), bf16[32,36,2048]{2,1,0:T(8,128)(2,1)}, u32[]{:S(2)}, u32[]{:S(2)}) async-start(bf16[32,36,2048]{2,1,0:T(8,128)(2,1)} %reshape.561), calls=%async_computation.3 | async-start | bytes 10485760 | tf_op jit(solution)/shard_map/all_to_all | solution.py:76
  426.6 120.8 %all-to-all-start.3 = ((bf16[32,36,2048]{2,1,0:T(8,128)(2,1)}), bf16[32,36,2048]{2,1,0:T(8,128)(2,1)}, u32[]{:S(2)}, u32[]{:S(2)}) async-start(bf16[32,36,2048]{2,1,0:T(8,128)(2,1)} %reshape.563), calls=%async_computation.4 | async-start | bytes 10485760 | tf_op jit(solution)/shard_map/all_to_all | solution.py:76
  547.3 120.8 %all-to-all-start.1 = ((bf16[32,36,2048]{2,1,0:T(8,128)(2,1)}), bf16[32,36,2048]{2,1,0:T(8,128)(2,1)}, u32[]{:S(2)}, u32[]{:S(2)}) async-start(bf16[32,36,2048]{2,1,0:T(8,128)(2,1)} %reshape.559), calls=%async_computation.2 | async-start | bytes 10485760 | tf_op jit(solution)/shard_map/all_to_all | solution.py:76
  553.7 190.8 %all-gather.7.cloned.1.call-start = ((), (), s32[]{:S(2)}) async-start(), calls=%async_computation.8 | async-start | bytes 2621440 | tf_op jit(solution)/shard_map/all_gather | solution.py:244
  697.1 163.1 %all-reduce.9.cloned.1.call-start = ((), (), s32[]{:S(2)}) async-start(), calls=%async_computation.10 | async-start | bytes 8388608 | tf_op jit(solution)/shard_map/psum | solution.py:334
  780.3 125.6 %reduce-scatter.5.cloned.1.call-start = ((), (), s32[]{:S(2)}) async-start(), calls=%async_computation.9 | async-start | bytes 2621440 | tf_op jit(solution)/shard_map/reduce_scatter | solution.py:316
  794.3 274.7 %all-gather.9.cloned.1.call-start = ((), (), s32[]{:S(2)}) async-start(), calls=%async_computation.11 | async-start | bytes 37748736 | tf_op jit(solution)/shard_map/all_gather | solution.py:16
  800.0 458.6 %all-reduce.11.cloned.1.call-start = ((), (), s32[]{:S(2)}) async-start(), calls=%async_computation.12 | async-start | bytes 17301504 | tf_op jit(solution)/shard_map/psum | solution.py:344
  838.3 67.7 %copy-start.46 = (f32[2048]{0:T(1024)S(1)}, f32[2048]{0:T(1024)}, u32[]{:S(2)}) copy-start(f32[2048]{0:T(1024)} %param.25) | copy-start | bytes 24580
  838.3 67.7 %copy-start.60 = (f32[128]{0:T(128)S(1)}, f32[128]{0:T(128)}, u32[]{:S(2)}) copy-start(f32[128]{0:T(128)} %copy-done.59) | copy-start | bytes 1540
  838.3 69.3 %copy-start.54 = (f32[2048]{0:T(1024)S(1)}, f32[2048]{0:T(1024)}, u32[]{:S(2)}) copy-start(f32[2048]{0:T(1024)} %get-tuple-element.58) | copy-start | bytes 24580
  838.3 69.3 %copy-start.70 = (f32[128]{0:T(128)S(1)}, f32[128]{0:T(128)}, u32[]{:S(2)}) copy-start(f32[128]{0:T(128)} %get-tuple-element.62) | copy-start | bytes 1540
  838.3 69.3 %copy-start.71 = (f32[128]{0:T(128)S(1)}, f32[128]{0:T(128)}, u32[]{:S(2)}) copy-start(f32[128]{0:T(128)} %get-tuple-element.54) | copy-start | bytes 1540
  838.3 110.3 %copy-start.73 = (f32[128]{0:T(128)S(1)}, f32[128]{0:T(128)}, u32[]{:S(2)}) copy-start(f32[128]{0:T(128)} %copy-done.72) | copy-start | bytes 1540
  838.3 110.3 %copy-start.11 = (f32[128,2048]{1,0:T(8,128)S(1)}, f32[128,2048]{1,0:T(8,128)}, u32[]{:S(2)}) copy-start(f32[128,2048]{1,0:T(8,128)} %copy-done.10) | copy-start | bytes 3145732
  838.3 110.3 %copy-start.18 = (bf16[128,2048]{1,0:T(8,128)(2,1)S(1)}, bf16[128,2048]{1,0:T(8,128)(2,1)}, u32[]{:S(2)}) copy-start(bf16[128,2048]{1,0:T(8,128)(2,1)} %param.39) | copy-start | bytes 1572868
  838.3 110.3 %copy-start.44 = (f32[2048]{0:T(1024)S(1)}, f32[2048]{0:T(1024)}, u32[]{:S(2)}) copy-start(f32[2048]{0:T(1024)} %param.32) | copy-start | bytes 24580
  838.4 110.2 %copy-start.58 = (f32[128]{0:T(128)S(1)}, f32[128]{0:T(128)}, u32[]{:S(2)}) copy-start(f32[128]{0:T(128)} %copy-done.57) | copy-start | bytes 1540
  838.4 110.2 %copy-start.69 = (f32[128]{0:T(128)S(1)}, f32[128]{0:T(128)}, u32[]{:S(2)}) copy-start(f32[128]{0:T(128)} %copy-done.68) | copy-start | bytes 1540
  (74 other events, 714.5 us)
Sparse Core Ops, SparseCore 0:
  11.9 48.3 all-gather.4
  89.8 42.5 reduce-scatter.2
  697.2 47.2 all-gather.6
  780.5 79.6 all-reduce.8
  862.3 43.6 reduce-scatter.4
  908.3 160.5 all-gather.8
  1076.2 182.3 all-reduce.10
